TPU v7x, 32 devices: a whole 2x2x4 slice. The times are simulated.
32 devices in a mesh: img: 4 (over x, core), tp: 8 (over z, y).
Axes of the slice: x: 2, y: 2, z: 4, core: 2. Of those that a mesh axis runs over, the one named last changes fastest.
Arguments:
- patch_tokens: bfloat16 [4096, 1024], P(('img', 'tp')), may hold values from -12 to 12
- norm_gain: float32 [1024], replicated, may hold values from 0.1 to 1.9
- norm_bias: float32 [1024], replicated, may hold values from -3 to 3
- up_weight: bfloat16 [1024, 8192], P('img', 'tp'), may hold values from -0.1875 to 0.1875
- up_bias: float32 [8192], P('tp'), may hold values from -3 to 3
- down_weight: bfloat16 [8192, 4096], P('tp', 'img'), may hold values from -0.125 to 0.125
- down_bias: float32 [4096], replicated, may hold values from -3 to 3
Outputs:
- projected: bfloat16 [4096, 4096], P(('img', 'tp'))
All inputs are finite; a program needn't handle non-finite values.
Results may differ from a plain program's by a relative error of at most 0.014.
Values may be sent and summed in bfloat16 or wider, within the bound.
A program may use at most 128 MiB of HBM per device.

v0:
```python
import jax
import jax.numpy as jnp
from jax import lax
from jax.sharding import PartitionSpec as P


def on_device(patch_tokens, norm_gain, norm_bias, up_weight, up_bias, down_weight, down_bias):
    values = lax.all_gather(patch_tokens, "tp", axis=0, tiled=True).astype(jnp.float32)
    center = jnp.mean(values, axis=1, keepdims=True)
    spread = jnp.mean((values - center) ** 2, axis=1, keepdims=True)
    gathered = ((values - center) * lax.rsqrt(spread + 1e-05) * norm_gain + norm_bias).astype(
        jnp.bfloat16
    )
    summed = jnp.dot(
        gathered,
        lax.all_gather(up_weight, "img", axis=0, tiled=True),
        preferred_element_type=jnp.float32,
    )
    hidden = jax.nn.gelu(summed + up_bias).astype(jnp.bfloat16)
    down_full = lax.all_gather(down_weight, "img", axis=1, tiled=True)
    total = lax.psum_scatter(
        jnp.dot(hidden, down_full, preferred_element_type=jnp.float32).astype(jnp.bfloat16),
        "tp",
        scatter_dimension=0,
        tiled=True,
    ).astype(jnp.float32)
    return (total + down_bias).astype(jnp.bfloat16)


def solution(mesh):
    return jax.shard_map(
        on_device,
        mesh=mesh,
        in_specs=(P(("img", "tp"), None), P(), P(), P("img", "tp"), P("tp"), P("tp", "img"), P()),
        out_specs=P(("img", "tp"), None),
        check_vma=False,
    )
```

profile of v0, /device:TPU:0, one launch (start us, length us, event | category | flops | bytes accessed | tf_op | source)
XLA Modules:
  0.0 318.9 jit_solution(16244446734320534299)
XLA Ops:
  6.5 0.0 copy-start.2
  6.5 0.0 copy-start.3
  6.5 0.0 copy-start.4
  6.5 0.0 all-gather.4.cloned.1.call-start
  6.5 0.7 all-gather.4.cloned.1.call-update
  7.3 0.0 all-gather.6.cloned.1.call-start
  7.3 0.7 all-gather.6.cloned.1.call-update
  8.0 0.0 all-gather.8.cloned.1.call-start
  8.1 0.7 all-gather.8.cloned.1.call-update
  8.7 0.0 reduce-scatter.2.cloned.1.call-start
  8.8 52.5 %all-gather.4.cloned.1.call-done = bf16[1024,1024]{1,0:T(8,128)(2,1)} async-done(((bf16[128,1024]{1,0:T(8,128)(2,1)}), bf16[1024,1024]{1,0:T(8,128)(2,1)}) %all-gather.4.cloned.1.call-update) | async-done | bytes 2097168 | tf_op jit(solution)/shard_map/all_gather | solution.py:8
  61.3 0.0 copy-start
  61.3 2.1 convert_reduce_fusion
  63.4 2.3 fusion.2
  65.7 18.3 %all-gather.6.cloned.1.call-done = bf16[1024,1024]{1,0:T(8,128)(2,1)} async-done(((bf16[256,1024]{1,0:T(8,128)(2,1)}), bf16[1024,1024]{1,0:T(8,128)(2,1)}) %all-gather.6.cloned.1.call-update) | async-done | bytes 2097168 | tf_op jit(solution)/shard_map/all_gather | solution.py:16
  84.0 59.9 %all-gather.8.cloned.1.call-done = bf16[1024,4096]{1,0:T(8,128)(2,1)} async-done(((bf16[1024,1024]{1,0:T(8,128)(2,1)}), bf16[1024,4096]{1,0:T(8,128)(2,1)}) %all-gather.8.cloned.1.call-update) | async-done | bytes 8388624 | tf_op jit(solution)/shard_map/all_gather | solution.py:20
  143.9 0.0 copy-done.2
  143.9 0.0 copy-done.3
  143.9 0.0 copy-done.4
  143.9 0.0 copy-done
  143.9 18.4 %convolution_convert_fusion = bf16[1024,4096]{1,0:T(8,128)(2,1)} fusion(bf16[1024,4096]{1,0:T(8,128)(2,1)} %all-gather.8.cloned.1.call-done, bf16[1024,1024]{1,0:T(8,128)(2,1)} %all-gather.6.cloned.1.call-done, bf16[1024,1024]{1,0:T(8,128)(2,1)S(1)} %copy-done, f32[1024]{0:T(1024)S(1)} %copy-done.2, f32[1024]{0:T(1024)S(1)} %copy-done.3, ...), kind=kOutput, calls=%fused_computation | convolution fusion | flops 10758389760 | bytes 20992000 | tf_op jit(solution)/shard_map/dot_general | solution.py:22
  162.3 0.0 copy-start.1
  162.3 0.0 reduce-scatter.2.cloned.1.call-update
  162.3 147.6 %reduce-scatter.2.cloned.1.call-done = bf16[128,4096]{1,0:T(8,128)(2,1)} async-done(((bf16[1024,4096]{1,0:T(8,128)(2,1)}), bf16[128,4096]{1,0:T(8,128)(2,1)}) %reduce-scatter.2.cloned.1.call-update) | async-done | bytes 1048592 | tf_op jit(solution)/shard_map/reduce_scatter | solution.py:21
  309.9 0.0 copy-done.1
  310.0 2.4 add_convert_fusion
  (2 shorter events, 0.0 us)
Async XLA Ops:
  6.5 137.3 %copy-start.2 = (f32[1024]{0:T(1024)S(1)}, f32[1024]{0:T(1024)}, u32[]{:S(2)}) copy-start(f32[1024]{0:T(1024)} %param.11) | copy-start | bytes 12292
  6.5 137.3 %copy-start.3 = (f32[1024]{0:T(1024)S(1)}, f32[1024]{0:T(1024)}, u32[]{:S(2)}) copy-start(f32[1024]{0:T(1024)} %param.9) | copy-start | bytes 12292
  6.5 137.3 %copy-start.4 = (f32[1024]{0:T(1024)S(1)}, f32[1024]{0:T(1024)}, u32[]{:S(2)}) copy-start(f32[1024]{0:T(1024)} %param.8) | copy-start | bytes 12292
  6.5 54.8 %all-gather.4.cloned.1.call-start = ((), (), s32[]{:S(2)}) async-start(), calls=%async_computation.1 | async-start | bytes 2359296 | tf_op jit(solution)/shard_map/all_gather | solution.py:8
  7.3 76.7 %all-gather.6.cloned.1.call-start = ((), (), s32[]{:S(2)}) async-start(), calls=%async_computation.2 | async-start | bytes 2621440 | tf_op jit(solution)/shard_map/all_gather | solution.py:16
  8.0 135.8 %all-gather.8.cloned.1.call-start = ((), (), s32[]{:S(2)}) async-start(), calls=%async_computation.3 | async-start | bytes 10485760 | tf_op jit(solution)/shard_map/all_gather | solution.py:20
  8.7 301.2 %reduce-scatter.2.cloned.1.call-start = ((), (), s32[]{:S(2)}) async-start(), calls=%async_computation.4 | async-start | bytes 9437184 | tf_op jit(solution)/shard_map/reduce_scatter | solution.py:21
  61.3 82.6 %copy-start = (bf16[1024,1024]{1,0:T(8,128)(2,1)S(1)}, bf16[1024,1024]{1,0:T(8,128)(2,1)}, u32[]{:S(2)}) copy-start(bf16[1024,1024]{1,0:T(8,128)(2,1)} %all-gather.4.cloned.1.call-done) | copy-start | bytes 6291460
  162.3 147.7 %copy-start.1 = (f32[4096]{0:T(1024)S(1)}, f32[4096]{0:T(1024)}, u32[]{:S(2)}) copy-start(f32[4096]{0:T(1024)} %param.13) | copy-start | bytes 49156
Sparse Core Ops, SparseCore 0:
  9.5 51.7 all-gather.3
  62.9 21.0 all-gather.5
  85.6 58.2 all-gather.7
  162.4 147.4 reduce-scatter.1
where the time goes:
time: 319 us
  waiting for transfers between devices  280 us (88%)
  matrix products  18.4 us (6%)
  between operations  13.1 us (4%)
  other arithmetic  6.78 us (2%)
    reduce_scatter x1, waiting for transfers between devices, on_device(): lax.psum_scatter(jnp.dot(hidden, down_full, preferred_element_type=jnp.fl...  148 us
    all_gather x1, waiting for transfers between devices, on_device(): down_full = lax.all_gather(down_weight, 'img', axis=1, tiled=True)  59.9 us
    all_gather x1, waiting for transfers between devices, on_device(): lax.all_gather(patch_tokens, 'tp', axis=0, tiled=True).astype(jnp.float32)  52.5 us
    dot_general x1, matrix products, on_device(): jnp.dot(hidden, down_full, preferred_element_type=jnp.float32)  18.4 us
    all_gather x1, waiting for transfers between devices, on_device(): lax.all_gather(up_weight, 'img', axis=0, tiled=True)  18.3 us
  transfers between devices with their start and end apart: 4, of which 4 were waited for; matrix products, arithmetic and copies ran while one was open for 1% of the time, Pallas kernels for 0%

commit v1 on v0

--- a/solution.py
+++ b/solution.py
@@ -17,7 +17,12 @@
         preferred_element_type=jnp.float32,
     )
     hidden = jax.nn.gelu(summed + up_bias).astype(jnp.bfloat16)
-    down_full = lax.all_gather(down_weight, "img", axis=1, tiled=True)
+    ring = [down_weight]
+    for hop in range(3):
+        ring.append(lax.ppermute(ring[-1], "img", [(dev, (dev + 1) % 4) for dev in range(4)]))
+    down_full = jnp.roll(
+        jnp.concatenate(ring[::-1], axis=1), (lax.axis_index("img") + 1) * ring[0].shape[1], axis=1
+    )
     total = lax.psum_scatter(
         jnp.dot(hidden, down_full, preferred_element_type=jnp.float32).astype(jnp.bfloat16),
         "tp",

time: 319 us -> 291 us (0.912)
  waiting for transfers between devices: 280 us -> 234 us
  local copies, waits for them, and re-layouts: 0.02 us -> 18.7 us
    ppermute x0 -> x3, waiting for transfers between devices: none -> 81 us  [on_device(): lax.ppermute(ring[-1], 'img', [(dev, (dev + 1) % 4) for dev in range(4)])]
    all_gather x1 -> x0, waiting for transfers between devices: 59.9 us -> none  [on_device(): down_full = lax.all_gather(down_weight, 'img', axis=1, tiled=True)]
    all_gather x1, waiting for transfers between devices: 52.5 us -> 2.76 us  [on_device(): lax.all_gather(patch_tokens, 'tp', axis=0, tiled=True).astype(jnp.float32)]
    all_gather x1, waiting for transfers between devices: 18.3 us -> 0.01 us  [on_device(): lax.all_gather(up_weight, 'img', axis=0, tiled=True)]
    unnamed x10 -> x23, local copies, waits for them, and re-layouts: 0.02 us -> 17.2 us
  transfers between devices with their start and end apart: 4 -> 6, of which waited for: 4 -> 5; matrix products, arithmetic and copies ran while one was open for 1% -> 8% of each run, Pallas kernels for 0% -> 0%
where the time goes in v1:
time: 291 us
  waiting for transfers between devices  234 us (80%)
  local copies, waits for them, and re-layouts  18.7 us (6%)
  matrix products  18.4 us (6%)
  between operations  13.2 us (5%)
  other arithmetic  6.63 us (2%)
    reduce_scatter x1, waiting for transfers between devices, on_device(): lax.psum_scatter(jnp.dot(hidden, down_full, preferred_element_type=jnp.fl...  150 us
    ppermute x3, waiting for transfers between devices, on_device(): lax.ppermute(ring[-1], 'img', [(dev, (dev + 1) % 4) for dev in range(4)])  81 us
    dot_general x1, matrix products, on_device(): jnp.dot(hidden, down_full, preferred_element_type=jnp.float32)  18.4 us
    unnamed x23, local copies, waits for them, and re-layouts  17.2 us
  transfers between devices with their start and end apart: 6, of which 5 were waited for; matrix products, arithmetic and copies ran while one was open for 8% of the time, Pallas kernels for 0%

profile of v1, /device:TPU:0, one launch (start us, length us, event | category | flops | bytes accessed | tf_op | source)
XLA Modules:
  0.0 291.2 jit_solution(256004349083801211)
XLA Ops:
  6.5 0.0 all-gather.3.cloned.1.call-start
  6.5 0.5 collective-permute-start
  7.0 0.2 all-gather.3.cloned.1.call-update
  7.3 0.0 all-gather.5.cloned.1.call-start
  7.3 25.6 %collective-permute-done = bf16[1024,1024]{1,0:T(8,128)(2,1)S(1)} collective-permute-done((bf16[1024,1024]{1,0:T(8,128)(2,1)}, bf16[1024,1024]{1,0:T(8,128)(2,1)S(1)}, u32[]{:S(2)}, u32[]{:S(2)}) %collective-permute-start) | collective-permute-done | bytes 2097184 | tf_op jit(solution)/shard_map/ppermute | solution.py:22
  32.9 0.0 copy-start.2
  32.9 0.0 collective-permute-start.1
  32.9 25.5 %collective-permute-done.1 = bf16[1024,1024]{1,0:T(8,128)(2,1)} collective-permute-done((bf16[1024,1024]{1,0:T(8,128)(2,1)S(1)}, bf16[1024,1024]{1,0:T(8,128)(2,1)}, u32[]{:S(2)}, u32[]{:S(2)}) %collective-permute-start.1) | collective-permute-done | bytes 2097184 | tf_op jit(solution)/shard_map/ppermute | solution.py:22
  58.4 0.0 collective-permute-start.2
  58.4 0.0 all-gather.5.cloned.1.call-update
  58.5 0.0 reduce-scatter.2.cloned.1.call-start
  58.5 2.8 all-gather.3.cloned.1.call-done
  61.3 1.9 convert_reduce_fusion
  63.2 2.3 fusion.7
  65.5 29.9 %collective-permute-done.2 = bf16[1024,1024]{1,0:T(8,128)(2,1)} collective-permute-done((bf16[1024,1024]{1,0:T(8,128)(2,1)}, bf16[1024,1024]{1,0:T(8,128)(2,1)}, u32[]{:S(2)}, u32[]{:S(2)}) %collective-permute-start.2) | collective-permute-done | bytes 2097184 | tf_op jit(solution)/shard_map/ppermute | solution.py:22
  95.4 3.1 %constant_dynamic-update-slice_fusion.7 = bf16[1024,8192]{1,0:T(8,128)(2,1)} fusion(bf16[1024,1024]{1,0:T(8,128)(2,1)} %collective-permute-done.2), kind=kLoop, calls=%fused_computation.38 | loop fusion | bytes 4194304
  98.5 0.0 copy-start
  98.5 3.2 %constant_dynamic-update-slice_fusion.6 = bf16[1024,8192]{1,0:T(8,128)(2,1)} fusion(bf16[1024,8192]{1,0:T(8,128)(2,1)} %constant_dynamic-update-slice_fusion.7, bf16[1024,1024]{1,0:T(8,128)(2,1)} %collective-permute-done.1), kind=kLoop, calls=%fused_computation.37 | loop fusion | bytes 4194304
  101.8 0.0 copy-done.2
  101.8 1.5 constant_dynamic-update-slice_fusion.5
  103.3 0.0 copy-done
  103.3 1.5 constant_dynamic-update-slice_fusion.4
  104.8 0.0 copy-start.3
  104.8 3.3 %constant_dynamic-update-slice_fusion.3 = bf16[1024,8192]{1,0:T(8,128)(2,1)} fusion(bf16[1024,8192]{1,0:T(8,128)(2,1)} %constant_dynamic-update-slice_fusion.4, bf16[1024,1024]{1,0:T(8,128)(2,1)} %collective-permute-done.2), kind=kLoop, calls=%fused_computation.34 | loop fusion | bytes 4194304
  108.0 3.1 %constant_dynamic-update-slice_fusion.2 = bf16[1024,8192]{1,0:T(8,128)(2,1)} fusion(bf16[1024,8192]{1,0:T(8,128)(2,1)} %constant_dynamic-update-slice_fusion.3, bf16[1024,1024]{1,0:T(8,128)(2,1)} %collective-permute-done.1), kind=kLoop, calls=%fused_computation.33 | loop fusion | bytes 4194304
  111.2 0.0 copy-done.3
  111.2 0.0 copy-start.1
  111.2 0.0 copy-start.5
  111.2 0.0 copy-start.6
  111.2 0.0 copy-start.7
  111.2 1.5 constant_dynamic-update-slice_fusion.1
  112.7 1.5 constant_dynamic-update-slice_fusion
  114.2 0.0 all-gather.5.cloned.1.call-done
  114.2 0.0 copy-done.1
  114.2 0.0 copy-done.5
  114.2 0.0 copy-done.6
  114.2 0.0 copy-done.7
  114.2 18.4 %fusion.2 = bf16[1024,4096]{1,0:T(8,128)(2,1)} fusion(bf16[1024,8192]{1,0:T(8,128)(2,1)} %constant_dynamic-update-slice_fusion, s32[]{:T(128)S(6)} %select_n.14, f32[1024]{0:T(1024)S(1)} %copy-done.5, bf16[1024,1024]{1,0:T(8,128)(2,1)} %all-gather.5.cloned.1.call-done, bf16[1024,1024]{1,0:T(8,128)(2,1)S(1)} %copy-done.1, f32[1024]{0:T(1024)S(1)} %copy-done.6, ...), kind=kOutput, calls=%fused_computation.2 | convolution fusion | flops 10758389760 | bytes 20992004 | tf_op jit(solution)/shard_map/dot_general | solution.py:27
  132.6 0.0 copy-start.4
  132.6 0.0 reduce-scatter.2.cloned.1.call-update
  132.6 149.6 %reduce-scatter.2.cloned.1.call-done = bf16[128,4096]{1,0:T(8,128)(2,1)} async-done(((bf16[1024,4096]{1,0:T(8,128)(2,1)}), bf16[128,4096]{1,0:T(8,128)(2,1)}) %reduce-scatter.2.cloned.1.call-update) | async-done | bytes 1048592 | tf_op jit(solution)/shard_map/reduce_scatter | solution.py:26
  282.3 0.0 copy-done.4
  282.3 2.4 add_convert_fusion
  (2 shorter events, 0.0 us)
Async XLA Ops:
  6.5 54.8 %all-gather.3.cloned.1.call-start = ((), (), s32[]{:S(2)}) async-start(), calls=%async_computation.1 | async-start | bytes 2359296 | tf_op jit(solution)/shard_map/all_gather | solution.py:8
  6.5 26.3 %collective-permute-start = (bf16[1024,1024]{1,0:T(8,128)(2,1)}, bf16[1024,1024]{1,0:T(8,128)(2,1)S(1)}, u32[]{:S(2)}, u32[]{:S(2)}) collective-permute-start(bf16[1024,1024]{1,0:T(8,128)(2,1)} %param.12), channel_id=1, source_target_pairs={{0,8},{8,16},{16,24},{24,0},{1,9},{9,17},{17,25},{25,1},{2,10},{10... | collective-permute-start | bytes 6291464 | tf_op jit(solution)/shard_map/ppermute | solution.py:22
  7.3 106.9 %all-gather.5.cloned.1.call-start = ((), (), s32[]{:S(2)}) async-start(), calls=%async_computation.2 | async-start | bytes 2621440 | tf_op jit(solution)/shard_map/all_gather | solution.py:16
  32.9 68.9 %copy-start.2 = (bf16[1024,1024]{1,0:T(8,128)(2,1)}, bf16[1024,1024]{1,0:T(8,128)(2,1)S(1)}, u32[]{:S(2)}) copy-start(bf16[1024,1024]{1,0:T(8,128)(2,1)S(1)} %collective-permute-done) | copy-start | bytes 6291460
  32.9 25.6 %collective-permute-start.1 = (bf16[1024,1024]{1,0:T(8,128)(2,1)S(1)}, bf16[1024,1024]{1,0:T(8,128)(2,1)}, u32[]{:S(2)}, u32[]{:S(2)}) collective-permute-start(bf16[1024,1024]{1,0:T(8,128)(2,1)S(1)} %collective-permute-done), channel_id=1, source_target_pairs={{0,8},{8,16},{16,24},{24,0},{1,9},{9,17},{17,25},{25,1},{2,10},{10... | collective-permute-start | bytes 6291464 | tf_op jit(solution)/shard_map/ppermute | solution.py:22
  58.4 37.0 %collective-permute-start.2 = (bf16[1024,1024]{1,0:T(8,128)(2,1)}, bf16[1024,1024]{1,0:T(8,128)(2,1)}, u32[]{:S(2)}, u32[]{:S(2)}) collective-permute-start(bf16[1024,1024]{1,0:T(8,128)(2,1)} %collective-permute-done.1), channel_id=1, source_target_pairs={{0,8},{8,16},{16,24},{24,0},{1,9},{9,17},{17,25},{25,1},{2,10},{10... | collective-permute-start | bytes 6291464 | tf_op jit(solution)/shard_map/ppermute | solution.py:22
  58.5 223.8 %reduce-scatter.2.cloned.1.call-start = ((), (), s32[]{:S(2)}) async-start(), calls=%async_computation.3 | async-start | bytes 9437184 | tf_op jit(solution)/shard_map/reduce_scatter | solution.py:26
  98.5 4.7 %copy-start = (bf16[1024,1024]{1,0:T(8,128)(2,1)S(1)}, bf16[1024,1024]{1,0:T(8,128)(2,1)}, u32[]{:S(2)}) copy-start(bf16[1024,1024]{1,0:T(8,128)(2,1)} %param.12) | copy-start | bytes 6291460
  104.8 6.4 %copy-start.3 = (bf16[1024,1024]{1,0:T(8,128)(2,1)S(1)}, bf16[1024,1024]{1,0:T(8,128)(2,1)}, u32[]{:S(2)}) copy-start(bf16[1024,1024]{1,0:T(8,128)(2,1)} %copy-done.2) | copy-start | bytes 6291460
  111.2 3.0 %copy-start.1 = (bf16[1024,1024]{1,0:T(8,128)(2,1)S(1)}, bf16[1024,1024]{1,0:T(8,128)(2,1)}, u32[]{:S(2)}) copy-start(bf16[1024,1024]{1,0:T(8,128)(2,1)} %all-gather.3.cloned.1.call-done) | copy-start | bytes 6291460
  111.2 3.0 %copy-start.5 = (f32[1024]{0:T(1024)S(1)}, f32[1024]{0:T(1024)}, u32[]{:S(2)}) copy-start(f32[1024]{0:T(1024)} %param.11) | copy-start | bytes 12292
  111.2 3.0 %copy-start.6 = (f32[1024]{0:T(1024)S(1)}, f32[1024]{0:T(1024)}, u32[]{:S(2)}) copy-start(f32[1024]{0:T(1024)} %param.9) | copy-start | bytes 12292
  111.2 3.0 %copy-start.7 = (f32[1024]{0:T(1024)S(1)}, f32[1024]{0:T(1024)}, u32[]{:S(2)}) copy-start(f32[1024]{0:T(1024)} %param.8) | copy-start | bytes 12292
  132.6 149.7 %copy-start.4 = (f32[4096]{0:T(1024)S(1)}, f32[4096]{0:T(1024)}, u32[]{:S(2)}) copy-start(f32[4096]{0:T(1024)} %param.13) | copy-start | bytes 49156
Sparse Core Ops, SparseCore 0:
  9.5 51.7 all-gather.2
  62.9 26.8 all-gather.4
  132.7 149.4 reduce-scatter.1
